TPU v7x, 32 devices: a whole 2x2x4 slice. The times are simulated.
32 devices in a mesh: tm: 16 (over z, y, core), series: 2 (over x).
Axes of the slice: x: 2, y: 2, z: 4, core: 2. Of those that a mesh axis runs over, the one named last changes fastest.
Arguments:
- history: bfloat16 [4, 4096, 1024], P('series', 'tm'), may hold values from -36 to 36
- lengths: int32 [4], P('series'), may hold values from 512 to 4096
- head_window: int32 [16], replicated, may hold values from 32 to 512, as said below
- input_proj: bfloat16 [1024, 3072], replicated
- output_proj: bfloat16 [1024, 1024], replicated, may hold values from -0.1875 to 0.1875
- mixer_down: bfloat16 [1024, 512], replicated, may hold values from -0.1875 to 0.1875
- mixer_up: bfloat16 [512, 1024], replicated, may hold values from -0.25 to 0.25
- series_mix: bfloat16 [4, 4], replicated, may hold values from -3 to 3
Outputs:
- layer_out: bfloat16 [4, 4096, 1024], P('series', 'tm')
Inputs may be any that keep to these rules, and one draw needn't show every extreme that they name: `head_window`: some head has exactly 512.
All inputs are finite; a program needn't handle non-finite values.
Results may differ from a plain program's by a relative error of at most 0.0065.
Values may be sent and summed in bfloat16 or wider, within the bound.
No kernel may reach another device: no remote copies, remote signals or barrier semaphores. Data moves between devices by JAX's collectives and lax.ppermute only.
A program may use at most 128 MiB of HBM per device.

v0:
```python
import jax
import jax.numpy as jnp
from jax import lax
from jax.sharding import PartitionSpec as P

HEADS = 16
WINDOW = 512


def from_behind(block, axis, distance):
    devices = range(lax.axis_size(axis))
    route = [(i - distance, i) for i in devices if i - distance in devices]
    return lax.ppermute(block, axis, route)


def attend_series(queries, keys_values, length, head_window, query_first, key_first, patches):
    query_rows = queries.shape[0]
    model_width = queries.shape[1]
    key_rows = keys_values.shape[0]
    head_size = model_width // HEADS
    group_heads = min(4, HEADS)
    group_count = HEADS // group_heads
    group_width = group_heads * head_size
    query_pos = query_first + jnp.arange(query_rows, dtype=jnp.int32)
    key_pos = key_first + jnp.arange(key_rows, dtype=jnp.int32)
    key_valid = (key_pos >= patches - length) & (key_pos < patches)
    distance = jnp.abs(query_pos[:, None] - key_pos[None, :])

    def per_group(group_index):
        column = group_index * group_width
        group_queries = lax.dynamic_slice_in_dim(queries, column, group_width, 1).reshape(
            query_rows, group_heads, head_size
        )
        group_keys = lax.dynamic_slice_in_dim(keys_values, column, group_width, 1).reshape(
            key_rows, group_heads, head_size
        )
        group_values = lax.dynamic_slice_in_dim(
            keys_values, model_width + column, group_width, 1
        ).reshape(key_rows, group_heads, head_size)
        reaches = lax.dynamic_slice_in_dim(head_window, group_index * group_heads, group_heads, 0)
        scores = jnp.einsum(
            "qhd,khd->hqk", group_queries, group_keys, preferred_element_type=jnp.float32
        ) * head_size ** (-0.5)
        allowed = (distance[None, :, :] <= reaches[:, None, None]) & key_valid[None, None, :]
        scores = jnp.where(allowed, scores, -1e30)
        largest = jnp.max(scores, axis=-1, keepdims=True)
        weights = jnp.exp(scores - largest)
        totals = jnp.sum(weights, axis=-1)
        probabilities = weights.astype(jnp.bfloat16)
        combined = (
            jnp.einsum(
                "hqk,khd->qhd", probabilities, group_values, preferred_element_type=jnp.float32
            )
            / jnp.transpose(totals)[:, :, None]
        )
        return combined.reshape(query_rows, group_width)

    grouped = lax.map(per_group, jnp.arange(group_count, dtype=jnp.int32))
    combined = jnp.transpose(grouped, (1, 0, 2)).reshape(query_rows, model_width)
    query_valid = query_pos >= patches - length
    return jnp.where(query_valid[:, None], combined, 0.0).astype(jnp.bfloat16)


def on_device(
    history, lengths, head_window, input_proj, output_proj, mixer_down, mixer_up, series_mix
):
    local_series, local_patches, model_width = history.shape
    packed = jnp.einsum(
        "spd,de->spe", history, input_proj, preferred_element_type=jnp.float32
    ).astype(jnp.bfloat16)
    queries = packed[:, :, :model_width]
    keys_values = packed[:, :, model_width:]
    hops_count = -(-WINDOW // local_patches)
    earlier = []
    following = []
    kv_weight = input_proj[:, model_width:]
    for offset in range(1, hops_count + 1):
        before_rows = from_behind(history, "tm", offset)
        after_rows = from_behind(history, "tm", -offset)
        earlier.insert(
            0,
            jnp.einsum(
                "spd,de->spe", before_rows, kv_weight, preferred_element_type=jnp.float32
            ).astype(jnp.bfloat16),
        )
        following.append(
            jnp.einsum(
                "spd,de->spe", after_rows, kv_weight, preferred_element_type=jnp.float32
            ).astype(jnp.bfloat16)
        )
    context = jnp.concatenate(earlier + [keys_values] + following, axis=1)
    position = lax.axis_index("tm")
    patches = local_patches * lax.axis_size("tm")
    query_first = position * local_patches
    key_first = (position - hops_count) * local_patches

    def per_series(inputs):
        series_queries, series_context, length = inputs
        return attend_series(
            series_queries, series_context, length, head_window, query_first, key_first, patches
        )

    attended = lax.map(per_series, (queries, context, lengths))
    hidden = (
        history.astype(jnp.float32)
        + jnp.einsum("spd,de->spe", attended, output_proj, preferred_element_type=jnp.float32)
    ).astype(jnp.bfloat16)
    branch = jnp.einsum(
        "spd,dc->spc", hidden, mixer_down, preferred_element_type=jnp.float32
    ).astype(jnp.bfloat16)
    series_first = lax.axis_index("series") * local_series
    own_rows = lax.dynamic_slice_in_dim(series_mix, series_first, local_series, 0)
    combined = jnp.einsum(
        "ab,bpc->apc",
        own_rows,
        lax.all_gather(branch, "series", axis=0, tiled=True),
        preferred_element_type=jnp.float32,
    )
    combined = combined.astype(jnp.bfloat16)
    update = jnp.einsum("spc,cd->spd", combined, mixer_up, preferred_element_type=jnp.float32)
    return (hidden.astype(jnp.float32) + update).astype(jnp.bfloat16)


def solution(mesh):
    in_specs = (P("series", "tm", None), P("series"), P(), P(), P(), P(), P(), P())
    out_specs = P("series", "tm", None)
    return jax.shard_map(
        on_device, mesh=mesh, in_specs=in_specs, out_specs=out_specs, check_vma=False
    )
```

profile of v0, /device:TPU:0, one launch (start us, length us, event | category | flops | bytes accessed | tf_op | source)
XLA Modules:
  0.0 253.0 jit_solution(13896051567737535328)
XLA Ops:
  6.5 6.0 %collective-permute-start = (bf16[2,256,1024]{2,1,0:T(8,128)(2,1)}, bf16[2,256,1024]{2,1,0:T(8,128)(2,1)}, u32[]{:S(2)}, u32[]{:S(2)}) collective-permute-start(bf16[2,256,1024]{2,1,0:T(8,128)(2,1)} %param.12), channel_id=1, source_target_pairs={{0,4},{2,6},{4,8},{6,10},{8,12},{10,14},{12,16},{14,18},{16,20},{1... | collective-permute-start | bytes 3145736 | tf_op jit(solution)/shard_map/ppermute | solution.py:13
  12.5 2.5 collective-permute-start.1
  15.0 1.3 collective-permute-start.2
  16.3 1.3 collective-permute-start.3
  17.6 6.5 %fusion.22 = bf16[2,256,3072]{2,1,0:T(8,128)(2,1)S(1)} fusion(bf16[2,256,1024]{2,1,0:T(8,128)(2,1)} %param.12, bf16[1024,3072]{1,0:T(8,128)(2,1)} %param.15), kind=kOutput, calls=%fused_computation.29 | convolution fusion | flops 3222798336 | bytes 10485760 | tf_op jit(solution)/shard_map/spd,de->spe/dot_general | solution.py:68
  24.2 1.6 copy-done.2
  26.9 42.2 %collective-permute-done = bf16[2,256,1024]{2,1,0:T(8,128)(2,1)} collective-permute-done((bf16[2,256,1024]{2,1,0:T(8,128)(2,1)}, bf16[2,256,1024]{2,1,0:T(8,128)(2,1)}, u32[]{:S(2)}, u32[]{:S(2)}) %collective-permute-start) | collective-permute-done | bytes 1048608 | tf_op jit(solution)/shard_map/ppermute | solution.py:13
  69.1 5.0 %fusion.36 = bf16[2,1280,2048]{2,1,0:T(8,128)(2,1)S(1)} fusion(bf16[2,256,1024]{2,1,0:T(8,128)(2,1)} %collective-permute-done, bf16[1024,3072]{1,0:T(8,128)(2,1)} %param.15), kind=kOutput, calls=%fused_computation.39 | convolution fusion | flops 2148532224 | bytes 7340032 | tf_op jit(solution)/shard_map/spd,de->spe/dot_general | solution.py:82
  74.2 5.0 %fusion.42 = bf16[2,1280,2048]{2,1,0:T(8,128)(2,1)S(1)} fusion(bf16[2,1280,2048]{2,1,0:T(8,128)(2,1)S(1)} %fusion.36, bf16[2,256,1024]{2,1,0:T(8,128)(2,1)} %collective-permute-done.1, bf16[1024,3072]{1,0:T(8,128)(2,1)} %param.15), kind=kOutput, calls=%fused_computation.41 | convolution fusion | flops 2148532224 | bytes 7340032 | tf_op jit(solution)/shard_map/spd,de->spe/dot_general | solution.py:82
  79.4 3.6 %fusion.48 = bf16[2,1280,2048]{2,1,0:T(8,128)(2,1)S(1)} fusion(bf16[2,1280,2048]{2,1,0:T(8,128)(2,1)S(1)} %slice_dynamic-update-slice_fusion, bf16[2,256,1024]{2,1,0:T(8,128)(2,1)} %collective-permute-done.2, bf16[1024,3072]{1,0:T(8,128)(2,1)S(1)} %bitcast.116), kind=kOutput, calls=%fused_computation.43 | convolution fusion | flops 2148532224 | bytes 7340032 | tf_op jit(solution)/shard_map/spd,de->spe/dot_general | solution.py:87
  83.0 2.3 fusion.54
  85.3 4.0 %copy-done.1 = bf16[2,1280,2048]{2,1,0:T(8,128)(2,1)} copy-done((bf16[2,1280,2048]{2,1,0:T(8,128)(2,1)}, bf16[2,1280,2048]{2,1,0:T(8,128)(2,1)S(1)}, u32[]{:S(2)}) %copy-start.1) | copy-done | bytes 10485784
  89.3 118.7 %while.33 = (s32[]{:T(128)}, bf16[2,256,1024]{1,2,0:T(8,128)(2,1)}, s32[]{:T(128)}, s32[2]{0:T(128)S(1)}, bf16[2,256,1024]{2,1,0:T(8,128)(2,1)}, /*index=5*/bf16...) while((s32[]{:T(128)}, bf16[2,256,1024]{1,2,0:T(8,128)(2,1)}, ...), condition=%wide.region_5.6_spmd, body=%wide.region_0.5_spmd.sunk | while | flops 348394496 | bytes 47223572 | solution.py:103
  90.6 5.6 %constant_dynamic-slice_fusion.9 = bf16[1,1280,2048]{2,1,0:T(8,128)(2,1)} fusion(bf16[2,1280,2048]{2,1,0:T(8,128)(2,1)} %get-tuple-element.545, s32[]{:T(128)} %get-tuple-element.521), kind=kLoop, calls=%fused_computation.25.clone.1 | loop fusion | bytes 10485764 | tf_op jit(solution)/shard_map/while/body/jit(dynamic_index_in_dim)/dynamic_slice | solution.py:103
  96.2 7.9 %copy.26 = bf16[1,1280,2048]{1,2,0:T(8,128)(2,1)} copy(bf16[1,1280,2048]{2,1,0:T(8,128)(2,1)} %constant_dynamic-slice_fusion.9) | data formatting | bytes 10485760 | tf_op jit(solution)/shard_map/while/body/jit(dynamic_index_in_dim)/dynamic_slice | solution.py:103
  106.7 40.1 %while.34 = (s32[]{:T(128)}, bf16[4,256,256]{1,2,0:T(8,128)(2,1)}, s32[4]{0:T(128)}, bf16[1280,2048]{0,1:T(8,128)(2,1)}, s32[16]{0:T(128)}, /*index=5*/bf16[256,...) while((s32[]{:T(128)}, bf16[4,256,256]{1,2,0:T(8,128)(2,1)}, ...), condition=%wide.region_4.4_spmd.clone, body=%wide.region_1.3_spmd.clone.sunk | while | flops 348130304 | bytes 23098768 | solution.py:58
  106.7 1.2 dynamic_slice.82
  108.4 1.4 constant_dynamic-slice_fusion.11
  112.3 1.8 fusion.98
  116.7 1.2 dynamic_slice.82
  118.4 1.4 constant_dynamic-slice_fusion.11
  122.3 1.8 fusion.98
  126.7 1.2 dynamic_slice.82
  128.4 1.4 constant_dynamic-slice_fusion.11
  132.3 1.8 fusion.98
  136.7 1.2 dynamic_slice.82
  138.4 1.4 constant_dynamic-slice_fusion.11
  142.3 1.8 fusion.98
  146.7 1.9 fusion.92
  149.9 5.6 %constant_dynamic-slice_fusion.9 = bf16[1,1280,2048]{2,1,0:T(8,128)(2,1)} fusion(bf16[2,1280,2048]{2,1,0:T(8,128)(2,1)} %get-tuple-element.545, s32[]{:T(128)} %get-tuple-element.521), kind=kLoop, calls=%fused_computation.25.clone.1 | loop fusion | bytes 10485764 | tf_op jit(solution)/shard_map/while/body/jit(dynamic_index_in_dim)/dynamic_slice | solution.py:103
  155.5 7.9 %copy.26 = bf16[1,1280,2048]{1,2,0:T(8,128)(2,1)} copy(bf16[1,1280,2048]{2,1,0:T(8,128)(2,1)} %constant_dynamic-slice_fusion.9) | data formatting | bytes 10485760 | tf_op jit(solution)/shard_map/while/body/jit(dynamic_index_in_dim)/dynamic_slice | solution.py:103
  166.0 40.1 %while.34 = (s32[]{:T(128)}, bf16[4,256,256]{1,2,0:T(8,128)(2,1)}, s32[4]{0:T(128)}, bf16[1280,2048]{0,1:T(8,128)(2,1)}, s32[16]{0:T(128)}, /*index=5*/bf16[256,...) while((s32[]{:T(128)}, bf16[4,256,256]{1,2,0:T(8,128)(2,1)}, ...), condition=%wide.region_4.4_spmd.clone, body=%wide.region_1.3_spmd.clone.sunk | while | flops 348130304 | bytes 23098768 | solution.py:58
  166.0 1.2 dynamic_slice.82
  167.7 1.4 constant_dynamic-slice_fusion.11
  171.6 1.8 fusion.98
  176.0 1.2 dynamic_slice.82
  177.7 1.4 constant_dynamic-slice_fusion.11
  181.6 1.8 fusion.98
  187.8 1.4 constant_dynamic-slice_fusion.11
  191.6 1.8 fusion.98
  197.8 1.4 constant_dynamic-slice_fusion.11
  201.7 1.8 fusion.98
  206.1 1.9 fusion.92
  208.0 3.0 %add_convert_fusion.1 = bf16[2,256,1024]{2,1,0:T(8,128)(2,1)S(1)} fusion(bf16[2,256,1024]{2,1,0:T(8,128)(2,1)} %param.12, bf16[2,256,1024]{1,2,0:T(8,128)(2,1)} %get-tuple-element.223, bf16[1024,1024]{1,0:T(8,128)(2,1)S(1)} %copy-done), kind=kOutput, calls=%fused_computation.54 | convolution fusion | flops 1075314688 | bytes 5242880 | tf_op jit(solution)/shard_map/spd,de->spe/dot_general | solution.py:106
  211.9 1.5 convolution_convert_fusion
  213.5 27.6 %all-gather.2.cloned.1.call-done = bf16[4,256,512]{2,1,0:T(8,128)(2,1)} async-done(((bf16[2,256,512]{2,1,0:T(8,128)(2,1)}), bf16[4,256,512]{2,1,0:T(8,128)(2,1)}) %all-gather.2.cloned.1.call-update) | async-done | bytes 1048592 | tf_op jit(solution)/shard_map/all_gather | solution.py:116
  241.1 2.1 fusion.67
  243.2 2.9 %add_convert_fusion = bf16[2,256,1024]{2,1,0:T(8,128)(2,1)} fusion(bf16[2,256,1024]{2,1,0:T(8,128)(2,1)} %copy-done.8, bf16[512,1024]{1,0:T(8,128)(2,1)S(1)} %copy-done.5, bf16[2,256,512]{2,0,1:T(2,128)(2,1)S(1)} %fusion.67), kind=kOutput, calls=%fused_computation.53 | convolution fusion | flops 538443776 | bytes 3670016 | tf_op jit(solution)/shard_map/spc,cd->spd/dot_general | solution.py:120
  (103 shorter events, 47.3 us)
Async XLA Ops:
  6.5 201.5 %copy-start = (bf16[1024,1024]{1,0:T(8,128)(2,1)S(1)}, bf16[1024,1024]{1,0:T(8,128)(2,1)}, u32[]{:S(2)}) copy-start(bf16[1024,1024]{1,0:T(8,128)(2,1)} %param.16) | copy-start | bytes 6291460
  6.5 234.5 %all-gather.2.cloned.1.call-start = ((), (), s32[]{:S(2)}) async-start(), calls=%async_computation | async-start | bytes 1572864 | tf_op jit(solution)/shard_map/all_gather | solution.py:116
  6.5 62.6 %collective-permute-start = (bf16[2,256,1024]{2,1,0:T(8,128)(2,1)}, bf16[2,256,1024]{2,1,0:T(8,128)(2,1)}, u32[]{:S(2)}, u32[]{:S(2)}) collective-permute-start(bf16[2,256,1024]{2,1,0:T(8,128)(2,1)} %param.12), channel_id=1, source_target_pairs={{0,4},{2,6},{4,8},{6,10},{8,12},{10,14},{12,16},{14,18},{16,20},{1... | collective-permute-start | bytes 3145736 | tf_op jit(solution)/shard_map/ppermute | solution.py:13
  12.5 61.6 %collective-permute-start.1 = (bf16[2,256,1024]{2,1,0:T(8,128)(2,1)}, bf16[2,256,1024]{2,1,0:T(8,128)(2,1)}, u32[]{:S(2)}, u32[]{:S(2)}) collective-permute-start(bf16[2,256,1024]{2,1,0:T(8,128)(2,1)} %param.12), channel_id=1, source_target_pairs={{0,2},{2,4},{4,6},{6,8},{8,10},{10,12},{12,14},{14,16},{16,18},{18... | collective-permute-start | bytes 3145736 | tf_op jit(solution)/shard_map/ppermute | solution.py:13
  15.0 64.3 %collective-permute-start.2 = (bf16[2,256,1024]{2,1,0:T(8,128)(2,1)}, bf16[2,256,1024]{2,1,0:T(8,128)(2,1)}, u32[]{:S(2)}, u32[]{:S(2)}) collective-permute-start(bf16[2,256,1024]{2,1,0:T(8,128)(2,1)} %param.12), channel_id=1, source_target_pairs={{2,0},{4,2},{6,4},{8,6},{10,8},{12,10},{14,12},{16,14},{18,16},{20... | collective-permute-start | bytes 3145736 | tf_op jit(solution)/shard_map/ppermute | solution.py:13
  16.3 66.7 %collective-permute-start.3 = (bf16[2,256,1024]{2,1,0:T(8,128)(2,1)}, bf16[2,256,1024]{2,1,0:T(8,128)(2,1)S(1)}, u32[]{:S(2)}, u32[]{:S(2)}) collective-permute-start(bf16[2,256,1024]{2,1,0:T(8,128)(2,1)} %param.12), channel_id=1, source_target_pairs={{4,0},{6,2},{8,4},{10,6},{12,8},{14,10},{16,12},{18,14},{20,16},{2... | collective-permute-start | bytes 3145736 | tf_op jit(solution)/shard_map/ppermute | solution.py:13
  24.2 1.6 copy-start.2
  69.1 10.2 %slice-start = ((s8[6291456]{0:T(1024)(128)(4,1)}), s8[4194304]{0:T(1024)(128)(4,1)S(1)}, s32[]{:S(2)}) async-start(s8[6291456]{0:T(1024)(128)(4,1)} %bitcast.115), calls=%async_computation.1 | async-start | bytes 8388608
  74.1 5.0 %copy-start.3 = (bf16[2,256,3072]{2,1,0:T(8,128)(2,1)S(1)}, bf16[2,256,3072]{2,1,0:T(8,128)(2,1)}, u32[]{:S(2)}) copy-start(bf16[2,256,3072]{2,1,0:T(8,128)(2,1)} %copy-done.2) | copy-start | bytes 9437188
  74.1 5.2 %slice-start.1 = ((s8[6291456]{0:T(1024)(128)(4,1)}), s8[2097152]{0:T(1024)(128)(4,1)S(1)}, s32[]{:S(2)}) async-start(s8[6291456]{0:T(1024)(128)(4,1)} %bitcast.115), calls=%async_computation.2 | async-start | bytes 4194304
  83.0 6.4 %copy-start.7 = (s32[2]{0:T(128)S(1)}, s32[2]{0:T(128)}, u32[]{:S(2)}) copy-start(s32[2]{0:T(128)} %param.13) | copy-start | bytes 28
  85.3 4.0 %copy-start.1 = (bf16[2,1280,2048]{2,1,0:T(8,128)(2,1)}, bf16[2,1280,2048]{2,1,0:T(8,128)(2,1)S(1)}, u32[]{:S(2)}) copy-start(bf16[2,1280,2048]{2,1,0:T(8,128)(2,1)S(1)} %fusion.54) | copy-start | bytes 31457284
  208.0 4.0 %copy-start.4 = (bf16[1024,512]{1,0:T(8,128)(2,1)S(1)}, bf16[1024,512]{1,0:T(8,128)(2,1)}, u32[]{:S(2)}) copy-start(bf16[1024,512]{1,0:T(8,128)(2,1)} %param.17) | copy-start | bytes 3145732
  208.0 33.1 %copy-start.6 = (bf16[4,4]{1,0:T(4,128)(2,1)S(1)}, bf16[4,4]{1,0:T(4,128)(2,1)}, u32[]{:S(2)}) copy-start(bf16[4,4]{1,0:T(4,128)(2,1)} %param.19) | copy-start | bytes 100
  208.0 35.2 %copy-start.5 = (bf16[512,1024]{1,0:T(8,128)(2,1)S(1)}, bf16[512,1024]{1,0:T(8,128)(2,1)}, u32[]{:S(2)}) copy-start(bf16[512,1024]{1,0:T(8,128)(2,1)} %param.18) | copy-start | bytes 3145732
  211.0 1.0 copy-start.8
Sparse Core Ops, SparseCore 0:
  213.6 27.3 all-gather.1
where the time goes:
time: 255 us; the launch traced here: 253 us
  local copies, waits for them, and re-layouts  80 us (31%)
  waiting for transfers between devices  69.8 us (27%)
  matrix products  54.1 us (21%)
  other arithmetic  13.6 us (5%)
  between operations  13.6 us (5%)
  starting transfers between devices  11.1 us (4%)
  loops' own time  10.8 us (4%)
    ppermute x4, waiting for transfers between devices, from_behind(): return lax.ppermute(block, axis, route)  42.3 us
    dynamic_slice x10, local copies, waits for them, and re-layouts, on_device(): attended = lax.map(per_series, (queries, context, lengths))  32.4 us
    all_gather x1, waiting for transfers between devices, on_device(): lax.all_gather(branch, 'series', axis=0, tiled=True)  27.6 us
    dot_general x8, matrix products, per_group(): jnp.einsum('qhd,khd->hqk', group_queries, group_keys, preferred_element_t...  14.1 us
    ppermute x4, starting transfers between devices, from_behind(): return lax.ppermute(block, axis, route)  11.1 us
    dynamic_slice x8, local copies, waits for them, and re-layouts, per_group(): lax.dynamic_slice_in_dim(keys_values, column, group_width, 1)  11 us
    dot_general x2, matrix products, on_device(): jnp.einsum('spd,de->spe', before_rows, kv_weight, preferred_element_type=...  9.98 us
    another operation x2, loops' own time, attend_series(): grouped = lax.map(per_group, jnp.arange(group_count, dtype=jnp.int32))  9.47 us
  transfers between devices with their start and end apart: 5, of which 2 were waited for; matrix products, arithmetic and copies ran while one was open for 8% of the time, Pallas kernels for 0%

commit v1 on v0

--- a/solution.py
+++ b/solution.py
@@ -110,12 +110,20 @@
     ).astype(jnp.bfloat16)
     series_first = lax.axis_index("series") * local_series
     own_rows = lax.dynamic_slice_in_dim(series_mix, series_first, local_series, 0)
-    combined = jnp.einsum(
-        "ab,bpc->apc",
-        own_rows,
-        lax.all_gather(branch, "series", axis=0, tiled=True),
-        preferred_element_type=jnp.float32,
-    )
+    size, index, width = (lax.axis_size("series"), lax.axis_index("series"), branch.shape[0])
+    right = [(i_2, (i_2 + 1) % size) for i_2 in range(size)]
+    held, total = (branch, None)
+    for hop in range(size):
+        following_2 = lax.ppermute(held, "series", right) if hop < size - 1 else None
+        update_2 = jnp.einsum(
+            "ab,bpc->apc",
+            lax.dynamic_slice_in_dim(own_rows, (index - hop) % size * width, held.shape[0], axis=1),
+            held,
+            preferred_element_type=jnp.float32,
+        )
+        total = update_2 if total is None else total + update_2
+        held = following_2
+    combined = total
     combined = combined.astype(jnp.bfloat16)
     update = jnp.einsum("spc,cd->spd", combined, mixer_up, preferred_element_type=jnp.float32)
     return (hidden.astype(jnp.float32) + update).astype(jnp.bfloat16)

time: 255 us -> 231 us (0.906)
  the two profiles are of different devices: /device:TPU:0 before, /device:TPU:1 now
where the time goes in v1:
time: 231 us; the launch traced here: 229 us
  local copies, waits for them, and re-layouts  81.4 us (35%)
  matrix products  55.5 us (24%)
  waiting for transfers between devices  53.1 us (23%)
  other arithmetic  13.6 us (6%)
  starting transfers between devices  12.9 us (6%)
  loops' own time  12.4 us (5%)
    ppermute x4, waiting for transfers between devices, from_behind(): return lax.ppermute(block, axis, route)  46.3 us
    dynamic_slice x10, local copies, waits for them, and re-layouts, on_device(): attended = lax.map(per_series, (queries, context, lengths))  32.3 us
    dot_general x8, matrix products, per_group(): jnp.einsum('qhd,khd->hqk', group_queries, group_keys, preferred_element_t...  14.2 us
    ppermute x4, starting transfers between devices, from_behind(): return lax.ppermute(block, axis, route)  11.7 us
    another operation x2, loops' own time, attend_series(): grouped = lax.map(per_group, jnp.arange(group_count, dtype=jnp.int32))  11.3 us
    dynamic_slice x8, local copies, waits for them, and re-layouts, per_group(): lax.dynamic_slice_in_dim(keys_values, column, group_width, 1)  11 us
    dynamic_slice x8, local copies, waits for them, and re-layouts, attend_series(): grouped = lax.map(per_group, jnp.arange(group_count, dtype=jnp.int32))  10.5 us
    dot_general x2, matrix products, on_device(): jnp.einsum('spd,de->spe', before_rows, kv_weight, preferred_element_type=...  9.83 us
  transfers between devices with their start and end apart: 5, of which 3 were waited for; matrix products, arithmetic and copies ran while one was open for 10% of the time, Pallas kernels for 0%

profile of v1, /device:TPU:1, one launch (start us, length us, event | category | flops | bytes accessed | tf_op | source)
XLA Modules:
  0.0 229.2 jit_solution(18353838745938396333)
XLA Ops:
  0.0 5.1 %collective-permute-start = (bf16[2,256,1024]{2,1,0:T(8,128)(2,1)}, bf16[2,256,1024]{2,1,0:T(8,128)(2,1)}, u32[]{:S(2)}, u32[]{:S(2)}) collective-permute-start(bf16[2,256,1024]{2,1,0:T(8,128)(2,1)} %param.12), channel_id=1, source_target_pairs={{0,4},{2,6},{4,8},{6,10},{8,12},{10,14},{12,16},{14,18},{16,20},{1... | collective-permute-start | bytes 3145736 | tf_op jit(solution)/shard_map/ppermute | solution.py:13
  5.1 3.0 %collective-permute-start.1 = (bf16[2,256,1024]{2,1,0:T(8,128)(2,1)}, bf16[2,256,1024]{2,1,0:T(8,128)(2,1)}, u32[]{:S(2)}, u32[]{:S(2)}) collective-permute-start(bf16[2,256,1024]{2,1,0:T(8,128)(2,1)} %param.12), channel_id=1, source_target_pairs={{0,2},{2,4},{4,6},{6,8},{8,10},{10,12},{12,14},{14,16},{16,18},{18... | collective-permute-start | bytes 3145736 | tf_op jit(solution)/shard_map/ppermute | solution.py:13
  8.1 2.3 %collective-permute-start.2 = (bf16[2,256,1024]{2,1,0:T(8,128)(2,1)}, bf16[2,256,1024]{2,1,0:T(8,128)(2,1)}, u32[]{:S(2)}, u32[]{:S(2)}) collective-permute-start(bf16[2,256,1024]{2,1,0:T(8,128)(2,1)} %param.12), channel_id=1, source_target_pairs={{2,0},{4,2},{6,4},{8,6},{10,8},{12,10},{14,12},{16,14},{18,16},{20... | collective-permute-start | bytes 3145736 | tf_op jit(solution)/shard_map/ppermute | solution.py:13
  11.7 6.5 %fusion.22 = bf16[2,256,3072]{2,1,0:T(8,128)(2,1)S(1)} fusion(bf16[2,256,1024]{2,1,0:T(8,128)(2,1)} %param.12, bf16[1024,3072]{1,0:T(8,128)(2,1)} %param.15), kind=kOutput, calls=%fused_computation.29 | convolution fusion | flops 3222798336 | bytes 10485760 | tf_op jit(solution)/shard_map/spd,de->spe/dot_general | solution.py:68
  18.3 1.6 copy-done.2
  21.0 38.9 %collective-permute-done = bf16[2,256,1024]{2,1,0:T(8,128)(2,1)} collective-permute-done((bf16[2,256,1024]{2,1,0:T(8,128)(2,1)}, bf16[2,256,1024]{2,1,0:T(8,128)(2,1)}, u32[]{:S(2)}, u32[]{:S(2)}) %collective-permute-start) | collective-permute-done | bytes 1048608 | tf_op jit(solution)/shard_map/ppermute | solution.py:13
  59.9 5.0 %fusion.36 = bf16[2,1280,2048]{2,1,0:T(8,128)(2,1)S(1)} fusion(bf16[2,256,1024]{2,1,0:T(8,128)(2,1)} %collective-permute-done, bf16[1024,3072]{1,0:T(8,128)(2,1)} %param.15), kind=kOutput, calls=%fused_computation.39 | convolution fusion | flops 2148532224 | bytes 7340032 | tf_op jit(solution)/shard_map/spd,de->spe/dot_general | solution.py:82
  65.0 7.3 %collective-permute-done.1 = bf16[2,256,1024]{2,1,0:T(8,128)(2,1)} collective-permute-done((bf16[2,256,1024]{2,1,0:T(8,128)(2,1)}, bf16[2,256,1024]{2,1,0:T(8,128)(2,1)}, u32[]{:S(2)}, u32[]{:S(2)}) %collective-permute-start.1) | collective-permute-done | bytes 1048608 | tf_op jit(solution)/shard_map/ppermute | solution.py:13
  72.3 4.8 %fusion.42 = bf16[2,1280,2048]{2,1,0:T(8,128)(2,1)S(1)} fusion(bf16[2,1280,2048]{2,1,0:T(8,128)(2,1)S(1)} %fusion.36, bf16[2,256,1024]{2,1,0:T(8,128)(2,1)} %collective-permute-done.1, bf16[1024,3072]{1,0:T(8,128)(2,1)} %param.15), kind=kOutput, calls=%fused_computation.41 | convolution fusion | flops 2148532224 | bytes 7340032 | tf_op jit(solution)/shard_map/spd,de->spe/dot_general | solution.py:82
  77.4 3.6 %fusion.48 = bf16[2,1280,2048]{2,1,0:T(8,128)(2,1)S(1)} fusion(bf16[2,1280,2048]{2,1,0:T(8,128)(2,1)S(1)} %slice_dynamic-update-slice_fusion, bf16[2,256,1024]{2,1,0:T(8,128)(2,1)} %collective-permute-done.2, bf16[1024,3072]{1,0:T(8,128)(2,1)S(1)} %bitcast.119), kind=kOutput, calls=%fused_computation.43 | convolution fusion | flops 2148532224 | bytes 7340032 | tf_op jit(solution)/shard_map/spd,de->spe/dot_general | solution.py:87
  81.0 2.3 %fusion.54 = bf16[2,1280,2048]{2,1,0:T(8,128)(2,1)S(1)} fusion(bf16[2,1280,2048]{2,1,0:T(8,128)(2,1)S(1)} %fusion.48, bf16[2,256,1024]{2,1,0:T(8,128)(2,1)S(1)} %collective-permute-done.3, bf16[1024,3072]{1,0:T(8,128)(2,1)S(1)} %bitcast.119), kind=kOutput, calls=%fused_computation.45 | convolution fusion | flops 2148532224 | bytes 7340032 | tf_op jit(solution)/shard_map/spd,de->spe/dot_general | solution.py:87
  83.3 4.0 %copy-done.1 = bf16[2,1280,2048]{2,1,0:T(8,128)(2,1)} copy-done((bf16[2,1280,2048]{2,1,0:T(8,128)(2,1)}, bf16[2,1280,2048]{2,1,0:T(8,128)(2,1)S(1)}, u32[]{:S(2)}) %copy-start.1) | copy-done | bytes 10485784
  87.3 121.8 %while.33 = (s32[]{:T(128)}, bf16[2,256,1024]{1,2,0:T(8,128)(2,1)}, s32[]{:T(128)}, s32[2]{0:T(128)S(1)}, bf16[2,256,1024]{2,1,0:T(8,128)(2,1)}, /*index=5*/bf16...) while((s32[]{:T(128)}, bf16[2,256,1024]{1,2,0:T(8,128)(2,1)}, ...), condition=%wide.region_5.6_spmd, body=%wide.region_0.5_spmd.sunk | while | flops 348394496 | bytes 47223572 | solution.py:103
  88.5 5.6 %constant_dynamic-slice_fusion.9 = bf16[1,1280,2048]{2,1,0:T(8,128)(2,1)} fusion(bf16[2,1280,2048]{2,1,0:T(8,128)(2,1)} %get-tuple-element.537, s32[]{:T(128)} %get-tuple-element.513), kind=kLoop, calls=%fused_computation.25.clone.1 | loop fusion | bytes 10485764 | tf_op jit(solution)/shard_map/while/body/jit(dynamic_index_in_dim)/dynamic_slice | solution.py:103
  94.1 7.9 %copy.31 = bf16[1,1280,2048]{1,2,0:T(8,128)(2,1)} copy(bf16[1,1280,2048]{2,1,0:T(8,128)(2,1)} %constant_dynamic-slice_fusion.9) | data formatting | bytes 10485760 | tf_op jit(solution)/shard_map/while/body/jit(dynamic_index_in_dim)/dynamic_slice | solution.py:103
  104.6 41.6 %while.34 = (s32[]{:T(128)}, bf16[4,256,256]{1,2,0:T(8,128)(2,1)}, s32[4]{0:T(128)}, bf16[1280,2048]{0,1:T(8,128)(2,1)}, s32[16]{0:T(128)}, /*index=5*/bf16[256,...) while((s32[]{:T(128)}, bf16[4,256,256]{1,2,0:T(8,128)(2,1)}, ...), condition=%wide.region_4.4_spmd.clone, body=%wide.region_1.3_spmd.clone.sunk | while | flops 348130304 | bytes 23098768 | solution.py:58
  104.6 1.3 dynamic_slice.87
  106.7 1.4 constant_dynamic-slice_fusion.11
  110.6 1.8 fusion.99
  115.0 1.3 dynamic_slice.87
  117.1 1.4 constant_dynamic-slice_fusion.11
  121.0 1.8 fusion.99
  125.5 1.3 dynamic_slice.87
  127.5 1.4 constant_dynamic-slice_fusion.11
  131.5 1.8 fusion.99
  135.9 1.3 dynamic_slice.87
  137.9 1.4 constant_dynamic-slice_fusion.11
  141.9 1.8 fusion.99
  146.3 1.9 fusion.93
  149.4 5.6 %constant_dynamic-slice_fusion.9 = bf16[1,1280,2048]{2,1,0:T(8,128)(2,1)} fusion(bf16[2,1280,2048]{2,1,0:T(8,128)(2,1)} %get-tuple-element.537, s32[]{:T(128)} %get-tuple-element.513), kind=kLoop, calls=%fused_computation.25.clone.1 | loop fusion | bytes 10485764 | tf_op jit(solution)/shard_map/while/body/jit(dynamic_index_in_dim)/dynamic_slice | solution.py:103
  155.0 7.9 %copy.31 = bf16[1,1280,2048]{1,2,0:T(8,128)(2,1)} copy(bf16[1,1280,2048]{2,1,0:T(8,128)(2,1)} %constant_dynamic-slice_fusion.9) | data formatting | bytes 10485760 | tf_op jit(solution)/shard_map/while/body/jit(dynamic_index_in_dim)/dynamic_slice | solution.py:103
  165.5 41.6 %while.34 = (s32[]{:T(128)}, bf16[4,256,256]{1,2,0:T(8,128)(2,1)}, s32[4]{0:T(128)}, bf16[1280,2048]{0,1:T(8,128)(2,1)}, s32[16]{0:T(128)}, /*index=5*/bf16[256,...) while((s32[]{:T(128)}, bf16[4,256,256]{1,2,0:T(8,128)(2,1)}, ...), condition=%wide.region_4.4_spmd.clone, body=%wide.region_1.3_spmd.clone.sunk | while | flops 348130304 | bytes 23098768 | solution.py:58
  165.5 1.3 dynamic_slice.87
  167.6 1.4 constant_dynamic-slice_fusion.11
  171.5 1.8 fusion.99
  178.0 1.4 constant_dynamic-slice_fusion.11
  181.9 1.8 fusion.99
  188.4 1.4 constant_dynamic-slice_fusion.11
  192.4 1.8 fusion.99
  198.8 1.4 constant_dynamic-slice_fusion.11
  202.8 1.8 fusion.99
  207.2 1.9 fusion.93
  209.1 2.9 %add_convert_fusion.1 = bf16[2,256,1024]{2,1,0:T(8,128)(2,1)S(1)} fusion(bf16[2,256,1024]{2,1,0:T(8,128)(2,1)} %param.12, bf16[2,256,1024]{1,2,0:T(8,128)(2,1)} %get-tuple-element.223, bf16[1024,1024]{1,0:T(8,128)(2,1)S(1)} %copy-done), kind=kOutput, calls=%fused_computation.54 | convolution fusion | flops 1075314688 | bytes 5242880 | tf_op jit(solution)/shard_map/spd,de->spe/dot_general | solution.py:106
  213.0 1.5 convolution_convert_fusion
  215.7 1.8 fusion.71
  217.5 6.8 %collective-permute-done.4 = bf16[2,256,512]{2,1,0:T(8,128)(2,1)} collective-permute-done((bf16[2,256,512]{2,1,0:T(8,128)(2,1)}, bf16[2,256,512]{2,1,0:T(8,128)(2,1)}, u32[]{:S(2)}, u32[]{:S(2)}) %collective-permute-start.4) | collective-permute-done | bytes 524320 | tf_op jit(solution)/shard_map/ppermute | solution.py:117
  224.4 1.8 fusion.69
  226.2 3.0 %add_convert_fusion = bf16[2,256,1024]{2,1,0:T(8,128)(2,1)} fusion(bf16[2,256,1024]{2,1,0:T(8,128)(2,1)} %copy-done.5, bf16[512,1024]{1,0:T(8,128)(2,1)S(1)} %copy-done.4, f32[2,256,512]{2,0,1:T(2,128)S(1)} %fusion.69, f32[2,256,512]{2,0,1:T(2,128)S(1)} %fusion.71), kind=kOutput, calls=%fused_computation.53 | convolution fusion | flops 538968064 | bytes 5242880 | tf_op jit(solution)/shard_map/spc,cd->spd/dot_general | solution.py:128
  (103 shorter events, 51.5 us)
Async XLA Ops:
  0.0 209.1 %copy-start = (bf16[1024,1024]{1,0:T(8,128)(2,1)S(1)}, bf16[1024,1024]{1,0:T(8,128)(2,1)}, u32[]{:S(2)}) copy-start(bf16[1024,1024]{1,0:T(8,128)(2,1)} %param.16) | copy-start | bytes 6291460
  0.0 59.9 %collective-permute-start = (bf16[2,256,1024]{2,1,0:T(8,128)(2,1)}, bf16[2,256,1024]{2,1,0:T(8,128)(2,1)}, u32[]{:S(2)}, u32[]{:S(2)}) collective-permute-start(bf16[2,256,1024]{2,1,0:T(8,128)(2,1)} %param.12), channel_id=1, source_target_pairs={{0,4},{2,6},{4,8},{6,10},{8,12},{10,14},{12,16},{14,18},{16,20},{1... | collective-permute-start | bytes 3145736 | tf_op jit(solution)/shard_map/ppermute | solution.py:13
  5.1 67.2 %collective-permute-start.1 = (bf16[2,256,1024]{2,1,0:T(8,128)(2,1)}, bf16[2,256,1024]{2,1,0:T(8,128)(2,1)}, u32[]{:S(2)}, u32[]{:S(2)}) collective-permute-start(bf16[2,256,1024]{2,1,0:T(8,128)(2,1)} %param.12), channel_id=1, source_target_pairs={{0,2},{2,4},{4,6},{6,8},{8,10},{10,12},{12,14},{14,16},{16,18},{18... | collective-permute-start | bytes 3145736 | tf_op jit(solution)/shard_map/ppermute | solution.py:13
  8.1 69.3 %collective-permute-start.2 = (bf16[2,256,1024]{2,1,0:T(8,128)(2,1)}, bf16[2,256,1024]{2,1,0:T(8,128)(2,1)}, u32[]{:S(2)}, u32[]{:S(2)}) collective-permute-start(bf16[2,256,1024]{2,1,0:T(8,128)(2,1)} %param.12), channel_id=1, source_target_pairs={{2,0},{4,2},{6,4},{8,6},{10,8},{12,10},{14,12},{16,14},{18,16},{20... | collective-permute-start | bytes 3145736 | tf_op jit(solution)/shard_map/ppermute | solution.py:13
  10.4 70.6 %collective-permute-start.3 = (bf16[2,256,1024]{2,1,0:T(8,128)(2,1)}, bf16[2,256,1024]{2,1,0:T(8,128)(2,1)S(1)}, u32[]{:S(2)}, u32[]{:S(2)}) collective-permute-start(bf16[2,256,1024]{2,1,0:T(8,128)(2,1)} %param.12), channel_id=1, source_target_pairs={{4,0},{6,2},{8,4},{10,6},{12,8},{14,10},{16,12},{18,14},{20,16},{2... | collective-permute-start | bytes 3145736 | tf_op jit(solution)/shard_map/ppermute | solution.py:13
  18.3 1.7 copy-start.2
  59.9 17.4 %slice-start = ((s8[6291456]{0:T(1024)(128)(4,1)}), s8[4194304]{0:T(1024)(128)(4,1)S(1)}, s32[]{:S(2)}) async-start(s8[6291456]{0:T(1024)(128)(4,1)} %bitcast.118), calls=%async_computation | async-start | bytes 8388608
  64.9 12.2 %copy-start.3 = (bf16[2,256,3072]{2,1,0:T(8,128)(2,1)S(1)}, bf16[2,256,3072]{2,1,0:T(8,128)(2,1)}, u32[]{:S(2)}) copy-start(bf16[2,256,3072]{2,1,0:T(8,128)(2,1)} %copy-done.2) | copy-start | bytes 9437188
  65.0 12.4 %slice-start.1 = ((s8[6291456]{0:T(1024)(128)(4,1)}), s8[2097152]{0:T(1024)(128)(4,1)S(1)}, s32[]{:S(2)}) async-start(s8[6291456]{0:T(1024)(128)(4,1)} %bitcast.118), calls=%async_computation.1 | async-start | bytes 4194304
  81.0 6.3 %copy-start.8 = (s32[2]{0:T(128)S(1)}, s32[2]{0:T(128)}, u32[]{:S(2)}) copy-start(s32[2]{0:T(128)} %param.13) | copy-start | bytes 28
  83.3 4.0 %copy-start.1 = (bf16[2,1280,2048]{2,1,0:T(8,128)(2,1)}, bf16[2,1280,2048]{2,1,0:T(8,128)(2,1)S(1)}, u32[]{:S(2)}) copy-start(bf16[2,1280,2048]{2,1,0:T(8,128)(2,1)S(1)} %fusion.54) | copy-start | bytes 31457284
  209.1 3.9 %copy-start.6 = (bf16[1024,512]{1,0:T(8,128)(2,1)S(1)}, bf16[1024,512]{1,0:T(8,128)(2,1)}, u32[]{:S(2)}) copy-start(bf16[1024,512]{1,0:T(8,128)(2,1)} %param.17) | copy-start | bytes 3145732
  209.1 6.6 %copy-start.7 = (bf16[4,4]{1,0:T(4,128)(2,1)S(1)}, bf16[4,4]{1,0:T(4,128)(2,1)}, u32[]{:S(2)}) copy-start(bf16[4,4]{1,0:T(4,128)(2,1)} %param.19) | copy-start | bytes 100
  212.0 1.0 copy-start.5
  213.0 13.2 %copy-start.4 = (bf16[512,1024]{1,0:T(8,128)(2,1)S(1)}, bf16[512,1024]{1,0:T(8,128)(2,1)}, u32[]{:S(2)}) copy-start(bf16[512,1024]{1,0:T(8,128)(2,1)} %param.18) | copy-start | bytes 3145732
  214.5 9.9 %collective-permute-start.4 = (bf16[2,256,512]{2,1,0:T(8,128)(2,1)}, bf16[2,256,512]{2,1,0:T(8,128)(2,1)}, u32[]{:S(2)}, u32[]{:S(2)}) collective-permute-start(bf16[2,256,512]{2,1,0:T(8,128)(2,1)} %convolution_convert_fusion), channel_id=1, source_target_pairs={{0,1},{1,0},{2,3},{3,2},{4,5},{5,4},{6,7},{7,6},{8,9},{9,8},{10,11... | collective-permute-start | bytes 1572872 | tf_op jit(solution)/shard_map/ppermute | solution.py:117
